TPU v7x, 32 devices: a whole 2x2x4 slice. The times are simulated.
32 devices in a mesh: dp: 16 (over z, y, x), mp: 2 (over core).
Axes of the slice: x: 2, y: 2, z: 4, core: 2. Of those that a mesh axis runs over, the one named last changes fastest.
Arguments:
- attn: bfloat16 [6144, 1536], P('dp', 'mp'), may hold values from -6 to 6
- w_out: bfloat16 [1536, 1536], P('mp'), may hold values from -0.15625 to 0.15625
- resid: bfloat16 [6144, 1536], P('dp', 'mp'), may hold values from -6 to 6
- target: bfloat16 [6144, 1536], P('dp', 'mp'), may hold values from -6 to 6
- gate: float32 [48, 1536], P('dp', 'mp'), may hold values from -5 to 5
- bins: int32 [48], P('dp'), may hold values from 0 to 127
Outputs:
- grad_w_out: float32 [1536, 1536], P('dp', 'mp')
- grad_gate: float32 [48, 1536], P('dp', 'mp')
- bin_loss: float32 [128], replicated
All inputs are finite; a program needn't handle non-finite values.
Results may differ from a plain program's by a relative error of at most 0.0008.
Values may be sent and summed in bfloat16 or wider, within the bound.
A program may use at most 64 MiB of HBM per device.

v0:
```python
import math
import jax
import jax.numpy as jnp
from jax import lax
from jax.sharding import PartitionSpec as P

NBINS = 128
LOSS_SCALE = 4096.0


def bin_weights():
    centre = (jnp.arange(NBINS).astype(jnp.float32) + 0.5) / NBINS
    logit = jnp.log(centre) - jnp.log(1.0 - centre)
    return jnp.exp(-0.5 * logit * logit) / (math.sqrt(2.0 * math.pi) * centre * (1.0 - centre))


def shards(attn, w_out, resid, target, gate, bins):
    samples = bins.shape[0]
    tok_rows = attn.shape[0]
    per_sample = tok_rows // samples
    full_width = w_out.shape[1]
    own_cols = resid.shape[1]
    bin_ids = jnp.arange(NBINS, dtype=jnp.int32)
    one_hot = (bins[:, None] == bin_ids[None, :]).astype(jnp.float32)
    local_counts = jnp.sum(one_hot, axis=0)
    weights = bin_weights()
    counts = lax.psum(local_counts, "dp")
    whole_attn = lax.all_gather(attn, "mp", axis=1, tiled=True)
    partial_value = jnp.dot(attn, w_out, preferred_element_type=jnp.float32)
    projected = lax.psum_scatter(partial_value, "mp", scatter_dimension=1, tiled=True)
    proj_cube = projected.reshape(samples, per_sample, own_cols)
    hidden = (
        resid.reshape(samples, per_sample, own_cols).astype(jnp.float32)
        + gate[:, None, :] * proj_cube
    )
    error_cube = hidden - target.reshape(samples, per_sample, own_cols).astype(jnp.float32)
    sample_error = jnp.sum(error_cube * error_cube, axis=(1, 2)) / (per_sample * full_width)
    bin_part = jnp.sum(one_hot * sample_error[:, None], axis=0)
    sums = lax.psum(bin_part, ("dp", "mp"))
    floored = jnp.maximum(counts, 1.0)
    scale_bin = LOSS_SCALE * weights / floored
    coefficient = jnp.sum(one_hot * scale_bin[None, :], axis=1) * (2.0 / (per_sample * full_width))
    d_hidden = coefficient[:, None, None] * error_cube
    grad_gate = jnp.sum(d_hidden * proj_cube, axis=1)
    d_proj = (d_hidden * gate[:, None, :]).astype(jnp.bfloat16).reshape(tok_rows, own_cols)
    full_grad = lax.dot_general(
        whole_attn, d_proj, (((0,), (0,)), ((), ())), preferred_element_type=jnp.float32
    )
    grad_out = lax.psum_scatter(full_grad, "dp", scatter_dimension=0, tiled=True)
    bin_loss = weights * sums / floored
    return (grad_out, grad_gate, bin_loss)


def solution(mesh):
    return jax.shard_map(
        shards,
        mesh=mesh,
        in_specs=(
            P("dp", "mp"),
            P("mp", None),
            P("dp", "mp"),
            P("dp", "mp"),
            P("dp", "mp"),
            P("dp"),
        ),
        out_specs=(P("dp", "mp"), P("dp", "mp"), P()),
        check_vma=False,
    )
```

profile of v0, /device:TPU:0, one launch (start us, length us, event | category | flops | bytes accessed | tf_op | source)
XLA Modules:
  0.0 214.0 jit_solution(4137970757654208983)
XLA Ops:
  7.2 0.0 copy-start
  7.2 0.0 reduce-scatter.5.cloned.1.call-start
  7.2 1.6 copy-done
  8.8 3.6 %fusion.5 = f32[384,1536]{1,0:T(8,128)} fusion(bf16[384,768]{1,0:T(8,128)(2,1)} %param.6, bf16[768,1536]{1,0:T(8,128)(2,1)S(1)} %copy-done), kind=kOutput, calls=%fused_computation.21 | convolution fusion | flops 905969664 | bytes 5308416 | tf_op jit(solution)/shard_map/dot_general | solution.py:29
  12.4 0.0 reduce-scatter.5.cloned.1.call-update
  12.4 0.0 all-gather.2.cloned.1.call-start
  12.5 0.7 all-gather.2.cloned.1.call-update
  13.2 0.0 reduce-scatter.7.cloned.1.call-start
  13.2 0.1 convert_reduce_fusion
  13.3 43.5 %psum.14 = f32[128]{0:T(128)S(1)} all-reduce(f32[128]{0:T(128)S(1)} %convert_reduce_fusion), channel_id=1, replica_groups=mesh['dp'=16,'mp'=2] {'dp'}, use_global_device_ids=true, to_apply=%region_1.0 | all-reduce | flops 128 | bytes 1024 | tf_op jit(solution)/shard_map/psum | solution.py:27
  56.8 0.5 multiply_divide_fusion.1
  57.4 0.0 copy-start.2
  57.4 2.1 multiply_reduce_fusion
  59.5 0.1 bitcast_reduce_fusion
  59.6 0.6 select_reduce_fusion
  60.2 0.1 broadcast_bitcast_fusion
  60.3 1.1 fusion.2
  61.4 5.0 %convolution_bitcast_fusion = f32[1536,768]{0,1:T(8,128)} fusion(bf16[384,768]{1,0:T(8,128)(2,1)} %fusion.2, bf16[384,1536]{1,0:T(8,128)(2,1)} %all-gather.2.cloned.1.call-done), kind=kOutput, calls=%fused_computation | convolution fusion | flops 905969664 | bytes 6488064 | tf_op jit(solution)/shard_map/dot_general | solution.py:46
  66.4 6.1 %copy.12 = f32[1536,768]{1,0:T(8,128)} copy(f32[1536,768]{0,1:T(8,128)} %convolution_bitcast_fusion) | data formatting | bytes 9437184
  72.6 0.0 reduce-scatter.7.cloned.1.call-update
  72.6 37.9 %psum.15 = f32[128]{0:T(128)} all-reduce(f32[128]{0:T(128)} %get-tuple-element.12), channel_id=1, replica_groups=mesh['dp'=16,'mp'=2] {'dp','mp'}, use_global_device_ids=true, to_apply=%region_9.10 | all-reduce | flops 128 | bytes 1024 | tf_op jit(solution)/shard_map/psum | solution.py:39
  110.5 1.2 multiply_divide_fusion
  111.7 2.2 %multiply_reduce_fusion.1 = f32[3,768]{1,0:T(4,128)} fusion(f32[3,128,768]{2,1,0:T(8,128)S(1)} %bitcast.29, f32[3]{0:T(128)S(1)} %broadcast_multiply_fusion.1, f32[3,768]{1,0:T(4,128)S(1)} %copy-done.4, bf16[3,128,768]{2,1,0:T(8,128)(2,1)} %bitcast.31, bf16[3,128,768]{2,1,0:T(8,128)(2,1)} %bitcast.30), kind=kLoop, calls=%fused_computation.7 | loop fusion | flops 2356992 | bytes 2377740 | tf_op jit(solution)/shard_map/reduce_sum | solution.py:44
  113.9 93.5 %reduce-scatter.7.cloned.1.call-done = f32[96,768]{1,0:T(8,128)} async-done(((f32[1536,768]{1,0:T(8,128)}), f32[96,768]{1,0:T(8,128)}) %reduce-scatter.7.cloned.1.call-update) | async-done | bytes 294928
  (17 shorter events, 0.0 us)
Async XLA Ops:
  7.2 1.7 copy-start
  7.2 50.2 %reduce-scatter.5.cloned.1.call-start = ((), (), s32[]{:S(2)}) async-start(), calls=%async_computation.2 | async-start | bytes 3538944 | tf_op jit(solution)/shard_map/reduce_scatter | solution.py:30
  12.4 0.8 copy-start.5
  12.4 45.0 %copy-start.4 = (f32[3,768]{1,0:T(4,128)S(1)}, f32[3,768]{1,0:T(4,128)}, u32[]{:S(2)}) copy-start(f32[3,768]{1,0:T(4,128)} %param.10) | copy-start | bytes 27652
  12.4 49.0 %all-gather.2.cloned.1.call-start = ((), (), s32[]{:S(2)}) async-start(), calls=%async_computation.3 | async-start | bytes 1769472 | tf_op jit(solution)/shard_map/all_gather | solution.py:28
  13.2 194.3 %reduce-scatter.7.cloned.1.call-start = ((), (), s32[]{:S(2)}) async-start(), calls=%async_computation.4 | async-start | bytes 5013504
  56.8 0.5 copy-start.7
  57.4 2.3 %copy-start.6 = (f32[128]{0:T(128)S(1)}, f32[128]{0:T(128)}, u32[]{:S(2)}) copy-start(f32[128]{0:T(128)} %multiply_divide_fusion.1) | copy-start | bytes 1540
  57.4 2.9 %copy-start.1 = (f32[384,768]{1,0:T(8,128)S(1)}, f32[384,768]{1,0:T(8,128)}, u32[]{:S(2)}) copy-start(f32[384,768]{1,0:T(8,128)} %reduce-scatter.5.cloned.1.call-done) | copy-start | bytes 3538948
  57.4 2.9 %copy-start.2 = (bf16[384,768]{1,0:T(8,128)(2,1)S(1)}, bf16[384,768]{1,0:T(8,128)(2,1)}, u32[]{:S(2)}) copy-start(bf16[384,768]{1,0:T(8,128)(2,1)} %param.9) | copy-start | bytes 1769476
  57.4 2.9 %copy-start.3 = (bf16[384,768]{1,0:T(8,128)(2,1)S(1)}, bf16[384,768]{1,0:T(8,128)(2,1)}, u32[]{:S(2)}) copy-start(bf16[384,768]{1,0:T(8,128)(2,1)} %param.8) | copy-start | bytes 1769476
Sparse Core Ops, SparseCore 0:
  12.5 12.7 reduce-scatter.4
  26.8 10.5 all-gather.1
  72.7 134.7 reduce-scatter.6
where the time goes:
time: 214 us
  waiting for transfers between devices  94.3 us (44%)
  blocking collectives  81.4 us (38%)
  between operations  13.8 us (6%)
  matrix products  8.55 us (4%)
  other arithmetic  7.99 us (4%)
  local copies, waits for them, and re-layouts  7.85 us (4%)
    unnamed x4, waiting for transfers between devices  94.3 us
    psum x1, blocking collectives, shards(): counts = lax.psum(local_counts, 'dp')  43.5 us
    psum x1, blocking collectives, shards(): sums = lax.psum(bin_part, ('dp', 'mp'))  37.9 us
    unnamed x17, local copies, waits for them, and re-layouts  7.78 us
    dot_general x1, matrix products, shards(): lax.dot_general(whole_attn, d_proj, (((0,), (0,)), ((), ())), preferred_e...  4.99 us
  transfers between devices with their start and end apart: 3, of which 1 were waited for; matrix products, arithmetic and copies ran while one was open for 4% of the time, Pallas kernels for 0%

commit v1 on v0

--- a/solution.py
+++ b/solution.py
@@ -36,7 +36,7 @@
     error_cube = hidden - target.reshape(samples, per_sample, own_cols).astype(jnp.float32)
     sample_error = jnp.sum(error_cube * error_cube, axis=(1, 2)) / (per_sample * full_width)
     bin_part = jnp.sum(one_hot * sample_error[:, None], axis=0)
-    sums = lax.psum(bin_part, ("dp", "mp"))
+    sums = jnp.sum(lax.all_gather(bin_part, ("dp", "mp")), axis=0)
     floored = jnp.maximum(counts, 1.0)
     scale_bin = LOSS_SCALE * weights / floored
     coefficient = jnp.sum(one_hot * scale_bin[None, :], axis=1) * (2.0 / (per_sample * full_width))

time: 214 us -> 215 us (level)
    psum x1 -> x0, blocking collectives: 37.9 us -> none  [shards(): sums = lax.psum(bin_part, ('dp', 'mp'))]
    all_gather x0 -> x1, blocking collectives: none -> 37.7 us  [shards(): sums = jnp.sum(lax.all_gather(bin_part, ('dp', 'mp')), axis=0)]
    unnamed x17 -> x21, local copies, waits for them, and re-layouts: 7.78 us -> 8.25 us
where the time goes in v1:
time: 215 us; the launch traced here: 214 us
  waiting for transfers between devices  94 us (44%)
  blocking collectives  81.2 us (38%)
  between operations  13.8 us (6%)
  matrix products  8.59 us (4%)
  local copies, waits for them, and re-layouts  8.32 us (4%)
  other arithmetic  8.31 us (4%)
    unnamed x4, waiting for transfers between devices  94 us
    psum x1, blocking collectives, shards(): counts = lax.psum(local_counts, 'dp')  43.5 us
    all_gather x1, blocking collectives, shards(): sums = jnp.sum(lax.all_gather(bin_part, ('dp', 'mp')), axis=0)  37.7 us
    unnamed x21, local copies, waits for them, and re-layouts  8.25 us
    dot_general x1, matrix products, shards(): lax.dot_general(whole_attn, d_proj, (((0,), (0,)), ((), ())), preferred_e...  5.04 us
  transfers between devices with their start and end apart: 3, of which 1 were waited for; matrix products, arithmetic and copies ran while one was open for 4% of the time, Pallas kernels for 0%

profile of v1, /device:TPU:0, one launch (start us, length us, event | category | flops | bytes accessed | tf_op | source)
XLA Modules:
  0.0 214.3 jit_solution(12898686166609804845)
XLA Ops:
  7.2 0.0 reduce-scatter.5.cloned.1.call-start
  7.2 1.6 copy-done
  8.8 3.6 %fusion.5 = f32[384,1536]{1,0:T(8,128)} fusion(bf16[384,768]{1,0:T(8,128)(2,1)} %param.6, bf16[768,1536]{1,0:T(8,128)(2,1)S(1)} %copy-done), kind=kOutput, calls=%fused_computation.21 | convolution fusion | flops 905969664 | bytes 5308416 | tf_op jit(solution)/shard_map/dot_general | solution.py:29
  12.4 0.0 reduce-scatter.5.cloned.1.call-update
  12.4 0.0 all-gather.4.cloned.1.call-start
  12.5 0.7 all-gather.4.cloned.1.call-update
  13.2 0.0 reduce-scatter.7.cloned.1.call-start
  13.2 0.1 convert_reduce_fusion
  13.3 43.5 %psum.7 = f32[128]{0:T(128)S(1)} all-reduce(f32[128]{0:T(128)S(1)} %convert_reduce_fusion), channel_id=1, replica_groups=mesh['dp'=16,'mp'=2] {'dp'}, use_global_device_ids=true, to_apply=%region_1.0 | all-reduce | flops 128 | bytes 1024 | tf_op jit(solution)/shard_map/psum | solution.py:27
  56.8 0.5 multiply_divide_fusion.1
  57.4 2.1 multiply_reduce_fusion
  59.5 0.1 bitcast_reduce_fusion
  59.6 0.2 select_reduce_fusion
  59.8 0.6 copy-done.5
  60.4 0.1 broadcast_bitcast_fusion
  60.5 1.1 fusion.2
  61.6 5.0 %convolution_bitcast_fusion = f32[1536,768]{0,1:T(8,128)} fusion(bf16[384,768]{1,0:T(8,128)(2,1)} %fusion.2, bf16[384,1536]{1,0:T(8,128)(2,1)} %all-gather.4.cloned.1.call-done), kind=kOutput, calls=%fused_computation | convolution fusion | flops 905969664 | bytes 6488064 | tf_op jit(solution)/shard_map/dot_general | solution.py:46
  66.6 6.0 %copy.12 = f32[1536,768]{1,0:T(8,128)} copy(f32[1536,768]{0,1:T(8,128)} %convolution_bitcast_fusion) | data formatting | bytes 9437184
  72.7 0.0 reduce-scatter.7.cloned.1.call-update
  72.7 37.7 %all-gather.1 = f32[32,1,128]{2,1,0:T(1,128)} all-gather(f32[1,1,128]{2,1,0:T(1,128)S(1)} %bitcast.33), channel_id=2, replica_groups=mesh['dp'=16,'mp'=2] {'dp','mp'}, dimensions={0}, use_global_device_ids=true | all-gather | bytes 16896 | tf_op jit(solution)/shard_map/all_gather | solution.py:39
  110.4 0.8 reduce_sum.68
  111.1 1.2 multiply_divide_fusion
  112.3 2.2 %multiply_reduce_fusion.1 = f32[3,768]{1,0:T(4,128)} fusion(f32[3,128,768]{2,1,0:T(8,128)S(1)} %bitcast.30, f32[3]{0:T(128)} %copy-done.5, f32[3,768]{1,0:T(4,128)S(1)} %copy-done.4, bf16[3,128,768]{2,1,0:T(8,128)(2,1)} %bitcast.32, bf16[3,128,768]{2,1,0:T(8,128)(2,1)} %bitcast.31), kind=kLoop, calls=%fused_computation.7 | loop fusion | flops 2356992 | bytes 2377740 | tf_op jit(solution)/shard_map/reduce_sum | solution.py:44
  114.5 93.3 %reduce-scatter.7.cloned.1.call-done = f32[96,768]{1,0:T(8,128)} async-done(((f32[1536,768]{1,0:T(8,128)}), f32[96,768]{1,0:T(8,128)}) %reduce-scatter.7.cloned.1.call-update) | async-done | bytes 294928
  (22 shorter events, 0.1 us)
Async XLA Ops:
  7.2 1.7 copy-start
  7.2 50.2 %reduce-scatter.5.cloned.1.call-start = ((), (), s32[]{:S(2)}) async-start(), calls=%async_computation.2 | async-start | bytes 3538944 | tf_op jit(solution)/shard_map/reduce_scatter | solution.py:30
  12.4 0.8 copy-start.6
  12.4 45.0 %copy-start.4 = (f32[3,768]{1,0:T(4,128)S(1)}, f32[3,768]{1,0:T(4,128)}, u32[]{:S(2)}) copy-start(f32[3,768]{1,0:T(4,128)} %param.10) | copy-start | bytes 27652
  12.4 49.2 %all-gather.4.cloned.1.call-start = ((), (), s32[]{:S(2)}) async-start(), calls=%async_computation.3 | async-start | bytes 1769472 | tf_op jit(solution)/shard_map/all_gather | solution.py:28
  13.2 194.6 %reduce-scatter.7.cloned.1.call-start = ((), (), s32[]{:S(2)}) async-start(), calls=%async_computation.4 | async-start | bytes 5013504
  56.8 0.5 copy-start.9
  57.4 2.3 %copy-start.7 = (s32[3]{0:T(128)S(1)}, s32[3]{0:T(128)}, u32[]{:S(2)}) copy-start(s32[3]{0:T(128)} %param.11) | copy-start | bytes 40
  57.4 2.3 %copy-start.8 = (f32[128]{0:T(128)S(1)}, f32[128]{0:T(128)}, u32[]{:S(2)}) copy-start(f32[128]{0:T(128)} %multiply_divide_fusion.1) | copy-start | bytes 1540
  57.4 3.1 %copy-start.1 = (f32[384,768]{1,0:T(8,128)S(1)}, f32[384,768]{1,0:T(8,128)}, u32[]{:S(2)}) copy-start(f32[384,768]{1,0:T(8,128)} %reduce-scatter.5.cloned.1.call-done) | copy-start | bytes 3538948
  57.4 3.1 %copy-start.2 = (bf16[384,768]{1,0:T(8,128)(2,1)S(1)}, bf16[384,768]{1,0:T(8,128)(2,1)}, u32[]{:S(2)}) copy-start(bf16[384,768]{1,0:T(8,128)(2,1)} %param.9) | copy-start | bytes 1769476
  57.4 3.1 %copy-start.3 = (bf16[384,768]{1,0:T(8,128)(2,1)S(1)}, bf16[384,768]{1,0:T(8,128)(2,1)}, u32[]{:S(2)}) copy-start(bf16[384,768]{1,0:T(8,128)(2,1)} %param.8) | copy-start | bytes 1769476
  59.8 0.6 copy-start.5
Sparse Core Ops, SparseCore 0:
  12.5 12.7 reduce-scatter.4
  26.8 10.5 all-gather.3
  72.8 134.9 reduce-scatter.6
